TPU v7x, 32 devices: a whole 2x2x4 slice. The times are simulated.
32 devices in a mesh: fsdp: 8 (over z, x), tp: 4 (over y, core).
Axes of the slice: x: 2, y: 2, z: 4, core: 2. Of those that a mesh axis runs over, the one named last changes fastest.
Arguments:
- slopes_in: float32 [32, 128, 4096], P(None, 'fsdp', 'tp'), may hold values from -6 to 6
- moments_in: float32 [32, 128, 4096], P(None, 'fsdp', 'tp'), may hold values from -6 to 6
- weights_in: float32 [32, 128, 4096], P(None, 'fsdp', 'tp'), may hold values from -0.1875 to 0.1875
Outputs:
- new_weights: float32 [32, 128, 4096], P(None, 'fsdp', 'tp')
- new_momentum: float32 [32, 128, 4096], P(None, 'fsdp', 'tp')
All inputs are finite; a program needn't handle non-finite values.
Results may differ from a plain program's by a relative error of at most 0.00021.
Values sent between devices are 32-bit elements; how exact they have to be, the bound alone decides.
A program may use at most 128 MiB of HBM per device.

v0:
```python
import functools
import jax
import jax.numpy as jnp
from jax import lax
from jax.sharding import PartitionSpec as P

ITERS = 5
HIGH = lax.Precision.HIGHEST
hold_rate = 0.8
learn_rate = 1.0


def polynomial(gram):
    side = gram.shape[-1]
    eye = jnp.eye(side, dtype=gram.dtype)
    dot = functools.partial(jnp.einsum, "mij,mjk->mik", precision=HIGH)
    scale = lax.rsqrt(jnp.sum(gram * eye, axis=(1, 2), keepdims=True) + 1e-06)
    gram = gram * (scale * scale)
    total = None
    for step in range(ITERS):
        mixed = 3.4445 * eye - 4.775 * gram + 2.0315 * dot(gram, gram)
        total = mixed * scale if total is None else dot(mixed, total)
        if step < ITERS - 1:
            gram = dot(dot(mixed, gram), mixed)
    return total


def body(slopes_in, moments_in, weights_in):
    new_momentum = hold_rate * moments_in + slopes_in
    moved = lax.all_to_all(new_momentum, "fsdp", split_axis=0, concat_axis=1, tiled=True)
    gram = lax.psum(jnp.einsum("mik,mjk->mij", moved, moved, precision=HIGH), "tp")
    iterate = jnp.einsum("mij,mjk->mik", polynomial(gram), moved, precision=HIGH)
    back = lax.all_to_all(iterate, "fsdp", split_axis=1, concat_axis=0, tiled=True)
    new_weights = weights_in - learn_rate * back
    return (new_weights, new_momentum)


def solution(mesh):
    return jax.shard_map(
        body,
        mesh=mesh,
        in_specs=(P(None, "fsdp", "tp"), P(None, "fsdp", "tp"), P(None, "fsdp", "tp")),
        out_specs=(P(None, "fsdp", "tp"), P(None, "fsdp", "tp")),
        check_vma=False,
    )
```

profile of v0, /device:TPU:0, one launch (start us, length us, event | category | flops | bytes accessed | tf_op | source)
XLA Modules:
  0.0 175.6 jit_solution(531279541024470661)
XLA Ops:
  7.2 2.7 %multiply_add_fusion = f32[32,16,1024]{2,1,0:T(8,128)S(1)} fusion(f32[32,16,1024]{2,1,0:T(8,128)} %param.3, f32[32,16,1024]{2,1,0:T(8,128)} %param.4), kind=kLoop, calls=%fused_computation.1 | loop fusion | flops 1048576 | bytes 6291456 | tf_op jit(solution)/shard_map/add | solution.py:29
  9.9 55.3 %all_to_all.36 = f32[32,16,1024]{2,1,0:T(8,128)S(1)} all-to-all(f32[32,16,1024]{2,1,0:T(8,128)S(1)} %multiply_add_fusion), channel_id=1, replica_groups=mesh['fsdp'=8,'tp'=4] {'fsdp'}, dimensions={0} | all-to-all | bytes 4194304 | tf_op jit(solution)/shard_map/all_to_all | solution.py:30
  65.3 2.8 %fusion.16 = f32[4,128,128]{2,1,0:T(8,128)} fusion(f32[4,128,1024]{2,1,0:T(8,128)S(1)} %bitcast.43), kind=kOutput, calls=%fused_computation.26 | convolution fusion | flops 805306368 | bytes 2359296 | tf_op jit(solution)/shard_map/mik,mjk->mij/dot_general | solution.py:31
  68.2 31.4 %all-reduce.2.cloned.1.call-done = f32[4,128,128]{2,1,0:T(8,128)} async-done(((f32[4,128,128]{2,1,0:T(8,128)}), f32[4,128,128]{2,1,0:T(8,128)}) %all-reduce.2.cloned.1.call-update) | async-done | bytes 262160 | tf_op jit(solution)/shard_map/psum | solution.py:31
  99.6 1.1 multiply_reduce_fusion
  100.7 1.6 fusion.4
  102.3 1.4 fusion.8
  103.7 0.4 fusion.17
  104.5 0.4 fusion.18
  104.9 0.4 fusion.5
  105.3 0.4 fusion.19
  106.1 0.4 fusion.20
  106.5 0.4 fusion.24
  106.9 0.4 fusion.21
  107.7 0.4 fusion.22
  108.1 0.4 fusion.25
  108.5 0.4 fusion.23
  109.3 0.4 fusion.26
  109.7 1.9 %fusion.27 = f32[4,128,1024]{2,1,0:T(8,128)S(1)} fusion(f32[4,128,128]{2,1,0:T(8,128)S(1)} %fusion.26, f32[4,128,1024]{2,1,0:T(8,128)S(1)} %bitcast.44), kind=kOutput, calls=%fused_computation.37 | convolution fusion | flops 805306368 | bytes 4456448 | tf_op jit(solution)/shard_map/mij,mjk->mik/dot_general | solution.py:32
  111.6 1.4 copy.8
  113.0 52.5 %all_to_all.37 = f32[4,128,1024]{2,0,1:T(4,128)S(1)} all-to-all(f32[4,128,1024]{2,0,1:T(4,128)S(1)} %copy.8), channel_id=1, replica_groups=mesh['fsdp'=8,'tp'=4] {'fsdp'}, dimensions={1} | all-to-all | bytes 4194304 | tf_op jit(solution)/shard_map/all_to_all | solution.py:33
  165.4 1.2 copy.9
  166.6 0.4 copy-done.1
  167.0 1.7 bitcast_subtract_fusion
  (13 shorter events, 1.7 us)
Async XLA Ops:
  7.2 92.4 %all-reduce.2.cloned.1.call-start = ((), (), s32[]{:S(2)}) async-start(), calls=%async_computation.2 | async-start | bytes 524288 | tf_op jit(solution)/shard_map/psum | solution.py:31
  9.9 55.3 %copy-start = (f32[32,16,1024]{2,1,0:T(8,128)}, f32[32,16,1024]{2,1,0:T(8,128)S(1)}, u32[]{:S(2)}) copy-start(f32[32,16,1024]{2,1,0:T(8,128)S(1)} %multiply_add_fusion) | copy-start | bytes 6291460
  165.4 1.6 copy-start.1
Sparse Core Ops, SparseCore 0:
  68.2 31.3 all-reduce.1
where the time goes:
time: 176 us
  blocking collectives  108 us (61%)
  waiting for transfers between devices  31.5 us (18%)
  between operations  14.2 us (8%)
  matrix products  13.5 us (8%)
  other arithmetic  5.5 us (3%)
  local copies, waits for them, and re-layouts  3.08 us (2%)
    all_to_all x1, blocking collectives, body(): lax.all_to_all(new_momentum, 'fsdp', split_axis=0, concat_axis=1, tiled=T...  55.3 us
    all_to_all x1, blocking collectives, body(): lax.all_to_all(iterate, 'fsdp', split_axis=1, concat_axis=0, tiled=True)  52.5 us
    psum x1, waiting for transfers between devices, body(): lax.psum(jnp.einsum('mik,mjk->mij', moved, moved, precision=HIGH), 'tp')  31.4 us
    dot_general x8, matrix products, polynomial(): gram = dot(dot(mixed, gram), mixed)  4.15 us
  transfers between devices with their start and end apart: 1, of which 1 were waited for; matrix products, arithmetic and copies ran while one was open for 0% of the time, Pallas kernels for 0%

commit v1 on v0

--- a/solution.py
+++ b/solution.py
@@ -8,6 +8,12 @@
 HIGH = lax.Precision.HIGHEST
 hold_rate = 0.8
 learn_rate = 1.0
+
+
+def gather_and_add(value, axis):
+    parts = lax.all_gather(value, axis, axis=0, tiled=False)
+    result = parts.sum(axis=0)
+    return result
 
 
 def polynomial(gram):
@@ -28,7 +34,7 @@
 def body(slopes_in, moments_in, weights_in):
     new_momentum = hold_rate * moments_in + slopes_in
     moved = lax.all_to_all(new_momentum, "fsdp", split_axis=0, concat_axis=1, tiled=True)
-    gram = lax.psum(jnp.einsum("mik,mjk->mij", moved, moved, precision=HIGH), "tp")
+    gram = gather_and_add(jnp.einsum("mik,mjk->mij", moved, moved, precision=HIGH), "tp")
     iterate = jnp.einsum("mij,mjk->mik", polynomial(gram), moved, precision=HIGH)
     back = lax.all_to_all(iterate, "fsdp", split_axis=1, concat_axis=0, tiled=True)
     new_weights = weights_in - learn_rate * back

time: 176 us -> 160 us (0.909)
  waiting for transfers between devices: 31.5 us -> 15.9 us
  matrix products: 13.5 us -> 11.5 us
    psum x1 -> x0, waiting for transfers between devices: 31.4 us -> none  [body(): lax.psum(jnp.einsum('mik,mjk->mij', moved, moved, precision=HIGH), 'tp')]
    all_gather x0 -> x1, waiting for transfers between devices: none -> 15.9 us  [gather_and_add(): parts = lax.all_gather(value, axis, axis=0, tiled=False)]
where the time goes in v1:
time: 160 us
  blocking collectives  109 us (68%)
  waiting for transfers between devices  15.9 us (10%)
  between operations  14.2 us (9%)
  matrix products  11.5 us (7%)
  other arithmetic  5.86 us (4%)
  local copies, waits for them, and re-layouts  3.18 us (2%)
    all_to_all x1, blocking collectives, body(): lax.all_to_all(new_momentum, 'fsdp', split_axis=0, concat_axis=1, tiled=T...  55.3 us
    all_to_all x1, blocking collectives, body(): lax.all_to_all(iterate, 'fsdp', split_axis=1, concat_axis=0, tiled=True)  53.9 us
    all_gather x1, waiting for transfers between devices, gather_and_add(): parts = lax.all_gather(value, axis, axis=0, tiled=False)  15.9 us
    dot_general x8, matrix products, polynomial(): gram = dot(dot(mixed, gram), mixed)  3.2 us
  transfers between devices with their start and end apart: 1, of which 1 were waited for; matrix products, arithmetic and copies ran while one was open for 0% of the time, Pallas kernels for 0%

profile of v1, /device:TPU:0, one launch (start us, length us, event | category | flops | bytes accessed | tf_op | source)
XLA Modules:
  0.0 159.8 jit_solution(6086261484391665000)
XLA Ops:
  7.2 2.7 %multiply_add_fusion = f32[32,16,1024]{2,1,0:T(8,128)S(1)} fusion(f32[32,16,1024]{2,1,0:T(8,128)} %param.3, f32[32,16,1024]{2,1,0:T(8,128)} %param.4), kind=kLoop, calls=%fused_computation.1 | loop fusion | flops 1048576 | bytes 6291456 | tf_op jit(solution)/shard_map/add | solution.py:35
  9.9 55.3 %all_to_all.36 = f32[32,16,1024]{2,1,0:T(8,128)S(1)} all-to-all(f32[32,16,1024]{2,1,0:T(8,128)S(1)} %multiply_add_fusion), channel_id=1, replica_groups=mesh['fsdp'=8,'tp'=4] {'fsdp'}, dimensions={0} | all-to-all | bytes 4194304 | tf_op jit(solution)/shard_map/all_to_all | solution.py:36
  65.4 2.8 %fusion.16 = f32[4,128,128]{2,1,0:T(8,128)} fusion(f32[4,128,1024]{2,1,0:T(8,128)S(1)} %bitcast.44), kind=kOutput, calls=%fused_computation.26 | convolution fusion | flops 805306368 | bytes 2359296 | tf_op jit(solution)/shard_map/mik,mjk->mij/dot_general | solution.py:37
  68.3 15.9 %all-gather.3.cloned.1.call-done = f32[16,128,128]{2,1,0:T(8,128)} async-done(((f32[4,128,128]{2,1,0:T(8,128)}), f32[16,128,128]{2,1,0:T(8,128)}) %all-gather.3.cloned.1.call-update) | async-done | bytes 1048592 | tf_op jit(solution)/shard_map/all_gather | solution.py:14
  84.1 1.3 reduce_sum.18
  85.6 0.5 fusion.4
  86.1 0.4 fusion.8
  86.5 0.4 fusion.17
  87.3 0.4 fusion.18
  87.7 0.4 fusion.5
  88.1 0.4 fusion.19
  88.9 0.4 fusion.20
  89.3 0.4 fusion.24
  89.7 0.4 fusion.21
  90.5 0.4 fusion.22
  90.9 0.4 fusion.25
  91.3 0.4 fusion.23
  92.1 0.4 fusion.26
  92.5 1.9 %fusion.27 = f32[4,128,1024]{2,1,0:T(8,128)S(1)} fusion(f32[4,128,128]{2,1,0:T(8,128)S(1)} %fusion.26, f32[4,128,1024]{2,1,0:T(8,128)S(1)} %bitcast.45), kind=kOutput, calls=%fused_computation.37 | convolution fusion | flops 805306368 | bytes 4456448 | tf_op jit(solution)/shard_map/mij,mjk->mik/dot_general | solution.py:38
  94.4 1.4 copy.8
  95.8 53.9 %all_to_all.37 = f32[4,128,1024]{2,0,1:T(4,128)S(1)} all-to-all(f32[4,128,1024]{2,0,1:T(4,128)S(1)} %copy.8), channel_id=1, replica_groups=mesh['fsdp'=8,'tp'=4] {'fsdp'}, dimensions={1} | all-to-all | bytes 4194304 | tf_op jit(solution)/shard_map/all_to_all | solution.py:39
  149.7 1.2 copy.9
  150.9 0.4 copy-done.1
  151.3 1.7 %bitcast_subtract_fusion = f32[32,16,1024]{2,1,0:T(8,128)} fusion(f32[32,16,1024]{2,1,0:T(8,128)S(1)} %copy-done.1, f32[8,4,16,1024]{3,2,1,0:T(8,128)S(1)} %copy.9), kind=kLoop, calls=%fused_computation | loop fusion | flops 524288 | bytes 6291456 | tf_op jit(solution)/shard_map/sub | solution.py:40
  (14 shorter events, 2.0 us)
Async XLA Ops:
  7.2 77.0 %all-gather.3.cloned.1.call-start = ((), (), s32[]{:S(2)}) async-start(), calls=%async_computation.2 | async-start | bytes 1310720 | tf_op jit(solution)/shard_map/all_gather | solution.py:14
  9.9 55.3 %copy-start = (f32[32,16,1024]{2,1,0:T(8,128)}, f32[32,16,1024]{2,1,0:T(8,128)S(1)}, u32[]{:S(2)}) copy-start(f32[32,16,1024]{2,1,0:T(8,128)S(1)} %multiply_add_fusion) | copy-start | bytes 6291460
  149.7 1.6 copy-start.1
Sparse Core Ops, SparseCore 0:
  68.3 15.7 all-gather.2
